TPU v7x, 32 devices: a whole 2x2x4 slice. The times are simulated.
32 devices in a mesh: groups: 2 (over x), blk: 8 (over z, y), span: 2 (over core).
Axes of the slice: x: 2, y: 2, z: 4, core: 2. Of those that a mesh axis runs over, the one named last changes fastest.
Arguments:
- embeddings: bfloat16 [8192, 768], P(('groups', 'blk', 'span')), parts along dimension 0, may hold values from -6 to 6
- owner_ids: int32 [8192, 1], P(('groups', 'blk', 'span')), parts along dimension 0, may hold values from 0 to 7, as said below
- local_ids: int32 [8192], P(('groups', 'blk', 'span')), parts along dimension 0, may hold values from 0 to 15, as said below
- cluster_map: int32 [256], P('groups'), parts along dimension 0, may hold values from 0 to 127, as said below
Outputs:
- nearest: float32 [8192], P(('groups', 'blk', 'span')), parts along dimension 0
- centroid_cosine: float32 [8192], P(('groups', 'blk', 'span')), parts along dimension 0
There are 2 independent parts, one for each index of `groups`. A program takes and returns all parts, laid end to end along the dimension named above; each array names one. Nothing has to cross between parts.
Inputs may be any that keep to these rules, and one draw needn't show every extreme that they name: `owner_ids`: at most 64 rows of one device name the same owner; in every draw one owner is named by exactly 64 rows of every device. `local_ids`: of the rows of one device that name one owner, at most 16 have local id 0; in every draw one owner receives exactly 16 rows with local id 0 from every device. In every draw some clusters with a local id other than 0 have exactly one row in the whole shard. cluster_map[o * 16 + l] = o * 16 + l for l > 0. For l = 0 the owners fall into runs of 1 to 3 consecutive owners, and every owner of a run has the value of the run's first owner; some run has 3 owners.
All inputs are finite; a program needn't handle non-finite values.
Results may differ from a plain program's by a relative error of at most 0.0017.
Values may be sent and summed in bfloat16 or wider, within the bound.
No kernel may reach another device: no remote copies, remote signals or barrier semaphores. Data moves between devices by JAX's collectives and lax.ppermute only.
A program may use at most 64 MiB of HBM per device.

v0:
```python
import jax
import jax.numpy as jnp
from jax import lax
from jax.sharding import PartitionSpec as P

GIANT_SPAN = 3


def passed_along(value, axis, steps):
    count = lax.axis_size(axis)
    first, last = (max(0, -steps), min(count, count - steps))
    return lax.ppermute(value, axis, [(source, source + steps) for source in range(first, last)])


def normalize(values):
    wide = values.astype(jnp.float32)
    scale = lax.rsqrt(jnp.sum(wide * wide, axis=1, keepdims=True) + 1e-06)
    return (wide * scale).astype(jnp.bfloat16)


def masked_scores(left, left_tags, right, right_tags):
    scores = lax.dot_general(
        left, right, (((1,), (1,)), ((), ())), preferred_element_type=jnp.float32
    )
    same = (left_tags[:, None] == right_tags[None, :]) & (left_tags[:, None] > 0)
    return jnp.where(same, scores, -1.0)


def body(embeddings, owner_ids, local_ids, cluster_map):
    rows = embeddings.shape[0]
    width = embeddings.shape[1]
    owners = lax.axis_size("blk")
    capacity = 2 * rows // owners
    slots = owners * capacity
    clusters = cluster_map.shape[0]
    owned = clusters // owners
    unit = normalize(embeddings)
    destination = owner_ids[:, 0]
    flat = destination * owned + local_ids
    table = jnp.arange(clusters, dtype=jnp.int32)
    cluster = jnp.sum(jnp.where(flat[:, None] == table[None, :], cluster_map[None, :], 0), axis=1)
    onehot = (destination[:, None] == jnp.arange(owners, dtype=jnp.int32)[None, :]).astype(
        jnp.int32
    )
    before = jnp.cumsum(onehot, axis=0) - onehot
    rank = jnp.sum(before * onehot, axis=1)
    position = destination * capacity + rank
    send_rows = jnp.zeros((slots, width), jnp.bfloat16).at[position].set(unit)
    send_tags = jnp.zeros((slots,), jnp.int32).at[position].set(cluster + 1)
    arrived, arrived_tags = (
        lax.all_to_all(
            send_rows.reshape(owners, capacity, width),
            "blk",
            split_axis=0,
            concat_axis=0,
            tiled=True,
        ),
        lax.all_to_all(
            send_tags.reshape(owners, capacity), "blk", split_axis=0, concat_axis=0, tiled=True
        ),
    )
    mine = arrived.reshape(slots, width)
    my_tags = arrived_tags.reshape(slots)
    chip, chip_tags = (
        lax.all_gather(mine, "span", axis=0, tiled=True),
        lax.all_gather(my_tags, "span", axis=0, tiled=True),
    )
    half = lax.axis_index("span")
    block_index = lax.axis_index("blk")
    own_tags = lax.dynamic_slice_in_dim(cluster_map, block_index * owned, owned, 0) + 1
    local = masked_scores(mine, my_tags, chip, chip_tags)
    itself = (
        jnp.arange(2 * slots, dtype=jnp.int32)[None, :]
        == (jnp.arange(slots, dtype=jnp.int32) + half * slots)[:, None]
    )
    best = jnp.max(jnp.where(itself, -1.0, local), axis=1)
    share_limit = 2 * owners * max(1, capacity // 4)
    shared_mask = chip_tags == own_tags[0]
    packed_rank = jnp.cumsum(shared_mask.astype(jnp.int32)) - 1
    target = jnp.where(shared_mask, packed_rank, share_limit)
    packed = jnp.zeros((share_limit, width), jnp.bfloat16).at[target].set(chip, mode="drop")
    packed_tags = jnp.zeros((share_limit,), jnp.int32).at[target].set(chip_tags, mode="drop")
    upper = (packed, packed_tags)
    lower = (packed, packed_tags)
    for step in range(1, GIANT_SPAN):
        upper = passed_along((upper[0], upper[1]), "blk", 1)
        lower = passed_along((lower[0], lower[1]), "blk", -1)
        for other in (upper, lower):
            best = jnp.maximum(
                best, jnp.max(masked_scores(mine, my_tags, other[0], other[1]), axis=1)
            )
    chosen = cluster[:, None] == table[None, :]
    partial_sums = lax.dot_general(
        chosen.astype(jnp.bfloat16),
        unit,
        (((0,), (0,)), ((), ())),
        preferred_element_type=jnp.float32,
    )
    sums = lax.psum(partial_sums, ("blk", "span"))
    length = jnp.sqrt(jnp.sum(sums * sums, axis=1, keepdims=True))
    direction = sums / jnp.maximum(length, 1.0)
    centroid_cosine = jnp.sum(unit.astype(jnp.float32) * direction[cluster], axis=1)
    returned_best = lax.all_to_all(
        best.reshape(owners, capacity), "blk", split_axis=0, concat_axis=0, tiled=True
    )
    nearest = returned_best.reshape(slots)[position]
    return (nearest, centroid_cosine)


def solution(mesh):
    return jax.shard_map(
        body,
        mesh=mesh,
        in_specs=(
            P(("groups", "blk", "span"), None),
            P(("groups", "blk", "span"), None),
            P(("groups", "blk", "span")),
            P("groups"),
        ),
        out_specs=(P(("groups", "blk", "span")), P(("groups", "blk", "span"))),
        check_vma=False,
    )
```

profile of v0, /device:TPU:0, one launch (start us, length us, event | category | flops | bytes accessed | tf_op | source)
XLA Modules:
  0.0 191.0 jit_solution(9322189716579336675)
XLA Ops:
  8.0 0.0 copy-start.3
  8.0 1.2 fusion
  9.2 0.7 fusion.10
  9.9 0.6 reduce-window.15
  10.5 0.2 slice_reduce_fusion
  10.8 0.8 fusion.9
  11.5 0.7 compare_select_fusion.2
  12.2 3.1 %scatter_custom_fusion.1 = bf16[512,768]{1,0:T(8,128)(2,1)} fusion(s32[256]{0:T(256)S(1)} %bitcast.54, bf16[]{:T(256)} %constant.23.clone.1, bf16[256,768]{1,0:T(8,128)(2,1)} %param.4, f32[256]{0:T(256)S(1)} %add_rsqrt_fusion), kind=kCustom, calls=%fused_computation.18 | custom fusion | flops 589824 | bytes 1180674 | tf_op jit(solution)/shard_map/scatter | solution.py:48
  15.3 7.3 %all-to-all-start.1 = ((bf16[8,64,768]{2,1,0:T(8,128)(2,1)}), bf16[8,64,768]{2,1,0:T(8,128)(2,1)S(1)}, u32[]{:S(2)}, u32[]{:S(2)}) async-start(bf16[8,64,768]{2,1,0:T(8,128)(2,1)} %bitcast.7), calls=%async_computation.1 | async-start | bytes 1572864 | tf_op jit(solution)/shard_map/all_to_all | solution.py:51
  22.6 0.0 all-reduce.2.cloned.1.call-start
  22.7 0.2 select_reduce_fusion.5
  22.9 1.1 fusion.6
  24.0 0.0 all-reduce.2.cloned.1.call-update
  24.1 1.4 scatter_custom_fusion
  25.5 0.7 all_to_all.13
  26.1 0.6 iota_add_fusion
  26.7 16.9 %all-to-all-done.1 = bf16[8,64,768]{2,1,0:T(8,128)(2,1)S(1)} async-done(((bf16[8,64,768]{2,1,0:T(8,128)(2,1)}), bf16[8,64,768]{2,1,0:T(8,128)(2,1)S(1)}, u32[]{:S(2)}, u32[]{:S(2)}) %all-to-all-start.1) | async-done | bytes 786464 | tf_op jit(solution)/shard_map/all_to_all | solution.py:51
  43.6 3.5 %all-to-all-start = ((s32[8,1,64]{2,1,0:T(1,128)}), s32[8,1,64]{2,1,0:T(1,128)S(1)}, u32[]{:S(2)}, u32[]{:S(2)}) async-start(s32[8,1,64]{2,1,0:T(1,128)} %all_to_all.13), calls=%async_computation | async-start | bytes 8192 | tf_op jit(solution)/shard_map/all_to_all | solution.py:58
  47.1 0.0 all-gather.3.cloned.1.call-start
  47.1 0.5 all-gather.3.cloned.1.call-update
  47.7 0.6 pad_clamp_fusion
  48.3 0.1 dynamic-slice_add_fusion
  48.3 5.2 %all-to-all-done = s32[8,1,64]{2,1,0:T(1,128)S(1)} async-done(((s32[8,1,64]{2,1,0:T(1,128)}), s32[8,1,64]{2,1,0:T(1,128)S(1)}, u32[]{:S(2)}, u32[]{:S(2)}) %all-to-all-start) | async-done | bytes 2080 | tf_op jit(solution)/shard_map/all_to_all | solution.py:58
  53.6 0.1 reshape.217
  53.7 1.8 all-gather
  55.5 0.3 reduce-window.19
  55.8 0.1 slice.19
  55.9 0.1 slice_reduce_fusion.1
  56.0 0.1 compare_select_fusion
  56.1 4.3 %scatter_custom_fusion.2 = s32[256]{0:T(256)S(1)} fusion(s32[1024]{0:T(1024)S(1)} %compare_select_fusion, s32[1024]{0:T(1024)S(1)} %bitcast.49, s32[]{:T(128)} %constant.19.clone.1), kind=kCustom, calls=%fused_computation.53 | custom fusion | bytes 1028 | tf_op jit(solution)/shard_map/scatter | solution.py:82
  60.4 1.3 collective-permute-start.2
  61.7 5.1 %collective-permute-start = (s32[256]{0:T(256)S(1)}, s32[256]{0:T(256)}, u32[]{:S(2)}, u32[]{:S(2)}) collective-permute-start(s32[256]{0:T(256)S(1)} %scatter_custom_fusion.2), channel_id=1, source_target_pairs={{0,2},{2,4},{4,6},{6,8},{8,10},{10,12},{12,14},{1,3},{3,5},{5,7},{... | collective-permute-start | bytes 3080 | tf_op jit(solution)/shard_map/ppermute | solution.py:12
  66.8 0.5 broadcast.121
  67.3 0.7 reduce.12
  68.0 0.1 eq.145
  68.1 0.5 broadcast_compare_fusion.1
  68.6 1.3 collective-permute-start.6
  69.9 5.1 %collective-permute-start.4 = (s32[256]{0:T(256)}, s32[256]{0:T(256)}, u32[]{:S(2)}, u32[]{:S(2)}) collective-permute-start(s32[256]{0:T(256)} %collective-permute-done), channel_id=1, source_target_pairs={{0,2},{2,4},{4,6},{6,8},{8,10},{10,12},{12,14},{1,3},{3,5},{5,7},{... | collective-permute-start | bytes 3080 | tf_op jit(solution)/shard_map/ppermute | solution.py:12
  75.0 47.2 %all-reduce.2.cloned.1.call-done = f32[128,768]{1,0:T(8,128)} async-done(((f32[128,768]{1,0:T(8,128)}), f32[128,768]{1,0:T(8,128)}) %all-reduce.2.cloned.1.call-update) | async-done | bytes 393232 | tf_op jit(solution)/shard_map/psum | solution.py:99
  122.2 1.1 multiply_reduce_fusion.1
  123.4 0.0 all-gather.3.cloned.1.call-done
  123.4 5.7 %scatter_custom_fusion.3 = bf16[256,768]{1,0:T(8,128)(2,1)S(1)} fusion(s32[1024]{0:T(1024)S(1)} %compare_select_fusion, bf16[1024,768]{1,0:T(8,128)(2,1)} %all-gather.3.cloned.1.call-done, bf16[]{:T(256)} %constant.23.clone.1), kind=kCustom, calls=%fused_computation.21 | custom fusion | bytes 393728 | tf_op jit(solution)/shard_map/scatter | solution.py:81
  129.1 1.3 collective-permute-start.3
  130.4 4.6 %collective-permute-start.1 = (bf16[256,768]{1,0:T(8,128)(2,1)S(1)}, bf16[256,768]{1,0:T(8,128)(2,1)S(1)}, u32[]{:S(2)}, u32[]{:S(2)}) collective-permute-start(bf16[256,768]{1,0:T(8,128)(2,1)S(1)} %scatter_custom_fusion.3), channel_id=1, source_target_pairs={{0,2},{2,4},{4,6},{6,8},{8,10},{10,12},{12,14},{1,3},{3,5},{5,7},{... | collective-permute-start | bytes 1179656 | tf_op jit(solution)/shard_map/ppermute | solution.py:12
  135.0 1.1 broadcast_divide_fusion
  136.1 1.4 gather_fusion.1
  137.5 2.8 %select_reduce_fusion = f32[512]{0:T(512)S(1)} fusion(bf16[512,768]{1,0:T(8,128)(2,1)S(1)} %bitcast.41, bf16[1024,768]{1,0:T(8,128)(2,1)} %all-gather.3.cloned.1.call-done, s32[1024]{0:T(1024)S(1)} %bitcast.50, s32[512]{0:T(512)} %iota_add_fusion, s32[512]{0:T(512)S(1)} %eq.145, pred[512]{0:T(512)(128)(4,1)} %broadcast_compare_fusion.1), kind=kOutput, calls=%fused_computation.6 | convolution fusion | flops 808451584 | bytes 2370048 | tf_op jit(solution)/shard_map/dot_general | solution.py:22
  140.3 0.7 collective-permute-done.3
  141.0 1.3 collective-permute-start.7
  142.3 6.2 %collective-permute-done.1 = bf16[256,768]{1,0:T(8,128)(2,1)S(1)} collective-permute-done((bf16[256,768]{1,0:T(8,128)(2,1)S(1)}, bf16[256,768]{1,0:T(8,128)(2,1)S(1)}, u32[]{:S(2)}, u32[]{:S(2)}) %collective-permute-start.1) | collective-permute-done | bytes 393248 | tf_op jit(solution)/shard_map/ppermute | solution.py:12
  148.5 4.4 %collective-permute-start.5 = (bf16[256,768]{1,0:T(8,128)(2,1)S(1)}, bf16[256,768]{1,0:T(8,128)(2,1)S(1)}, u32[]{:S(2)}, u32[]{:S(2)}) collective-permute-start(bf16[256,768]{1,0:T(8,128)(2,1)S(1)} %collective-permute-done.1), channel_id=1, source_target_pairs={{0,2},{2,4},{4,6},{6,8},{8,10},{10,12},{12,14},{1,3},{3,5},{5,7},{... | collective-permute-start | bytes 1179656 | tf_op jit(solution)/shard_map/ppermute | solution.py:12
  152.9 0.4 fusion.17
  153.3 0.4 fusion.18
  153.7 0.4 fusion.19
  154.1 11.3 %collective-permute-done.5 = bf16[256,768]{1,0:T(8,128)(2,1)S(1)} collective-permute-done((bf16[256,768]{1,0:T(8,128)(2,1)S(1)}, bf16[256,768]{1,0:T(8,128)(2,1)S(1)}, u32[]{:S(2)}, u32[]{:S(2)}) %collective-permute-start.5) | collective-permute-done | bytes 393248 | tf_op jit(solution)/shard_map/ppermute | solution.py:12
  165.4 1.3 select_reduce_fusion.4
  166.7 0.7 max.65
  167.4 5.9 %all-to-all-start.2 = ((f32[8,1,64]{2,1,0:T(1,128)}), f32[8,1,64]{2,1,0:T(1,128)S(1)}, u32[]{:S(2)}, u32[]{:S(2)}) async-start(f32[8,1,64]{2,1,0:T(1,128)} %max.65), calls=%async_computation.2 | async-start | bytes 8192 | tf_op jit(solution)/shard_map/all_to_all | solution.py:103
  173.3 0.8 multiply_reduce_fusion
  174.1 5.7 %all-to-all-done.2 = f32[8,1,64]{2,1,0:T(1,128)S(1)} async-done(((f32[8,1,64]{2,1,0:T(1,128)}), f32[8,1,64]{2,1,0:T(1,128)S(1)}, u32[]{:S(2)}, u32[]{:S(2)}) %all-to-all-start.2) | async-done | bytes 2080 | tf_op jit(solution)/shard_map/all_to_all | solution.py:103
  179.8 0.5 broadcast.122
  180.3 0.7 reduce.13
  181.0 0.1 reshape.165
  181.1 2.5 %gather_fusion = f32[256]{0:T(256)} fusion(f32[512]{0:T(512)S(1)} %reshape.165, s32[1024]{0:T(1024)S(1)} %pad_clamp_fusion.1), kind=kCustom, calls=%fused_computation | custom fusion | bytes 3072 | tf_op jit(solution)/shard_map/gather | solution.py:106
  (29 shorter events, 0.2 us)
Async XLA Ops:
  8.0 14.9 %copy-start.2 = (bf16[256,768]{1,0:T(8,128)(2,1)S(1)}, bf16[256,768]{1,0:T(8,128)(2,1)}, u32[]{:S(2)}) copy-start(bf16[256,768]{1,0:T(8,128)(2,1)} %param.4) | copy-start | bytes 1179652
  8.0 14.7 %copy-start.3 = (s32[256,1]{0,1:T(1,128)S(1)}, s32[256,1]{0,1:T(1,128)}, u32[]{:S(2)}) copy-start(s32[256,1]{0,1:T(1,128)} %param.5) | copy-start | bytes 3076
  8.0 14.7 %copy-start.4 = (s32[256]{0:T(256)S(1)}, s32[256]{0:T(256)}, u32[]{:S(2)}) copy-start(s32[256]{0:T(256)} %param.6) | copy-start | bytes 3076
  8.0 14.7 %copy-start.5 = (s32[128]{0:T(128)S(1)}, s32[128]{0:T(128)}, u32[]{:S(2)}) copy-start(s32[128]{0:T(128)} %param.7) | copy-start | bytes 1540
  15.3 28.3 %all-to-all-start.1 = ((bf16[8,64,768]{2,1,0:T(8,128)(2,1)}), bf16[8,64,768]{2,1,0:T(8,128)(2,1)S(1)}, u32[]{:S(2)}, u32[]{:S(2)}) async-start(bf16[8,64,768]{2,1,0:T(8,128)(2,1)} %bitcast.7), calls=%async_computation.1 | async-start | bytes 1572864 | tf_op jit(solution)/shard_map/all_to_all | solution.py:51
  22.6 99.6 %all-reduce.2.cloned.1.call-start = ((), (), s32[]{:S(2)}) async-start(), calls=%async_computation.4 | async-start | bytes 786432 | tf_op jit(solution)/shard_map/psum | solution.py:99
  43.6 3.5 %copy-start = (bf16[8,64,768]{2,1,0:T(8,128)(2,1)}, bf16[8,64,768]{2,1,0:T(8,128)(2,1)S(1)}, u32[]{:S(2)}) copy-start(bf16[8,64,768]{2,1,0:T(8,128)(2,1)S(1)} %all-to-all-done.1) | copy-start | bytes 2359300
  43.6 10.0 %all-to-all-start = ((s32[8,1,64]{2,1,0:T(1,128)}), s32[8,1,64]{2,1,0:T(1,128)S(1)}, u32[]{:S(2)}, u32[]{:S(2)}) async-start(s32[8,1,64]{2,1,0:T(1,128)} %all_to_all.13), calls=%async_computation | async-start | bytes 8192 | tf_op jit(solution)/shard_map/all_to_all | solution.py:58
  47.1 76.3 %all-gather.3.cloned.1.call-start = ((), (), s32[]{:S(2)}) async-start(), calls=%async_computation.3 | async-start | bytes 2359296 | tf_op jit(solution)/shard_map/all_gather | solution.py:65
  60.4 8.2 %collective-permute-start.2 = (s32[256]{0:T(256)S(1)}, s32[256]{0:T(256)}, u32[]{:S(2)}, u32[]{:S(2)}) collective-permute-start(s32[256]{0:T(256)S(1)} %scatter_custom_fusion.2), channel_id=1, source_target_pairs={{2,0},{4,2},{6,4},{8,6},{10,8},{12,10},{14,12},{3,1},{5,3},{7,5},{... | collective-permute-start | bytes 3080 | tf_op jit(solution)/shard_map/ppermute | solution.py:12
  61.7 8.2 %collective-permute-start = (s32[256]{0:T(256)S(1)}, s32[256]{0:T(256)}, u32[]{:S(2)}, u32[]{:S(2)}) collective-permute-start(s32[256]{0:T(256)S(1)} %scatter_custom_fusion.2), channel_id=1, source_target_pairs={{0,2},{2,4},{4,6},{6,8},{8,10},{10,12},{12,14},{1,3},{3,5},{5,7},{... | collective-permute-start | bytes 3080 | tf_op jit(solution)/shard_map/ppermute | solution.py:12
  68.6 85.5 %collective-permute-start.6 = (s32[256]{0:T(256)}, s32[256]{0:T(256)}, u32[]{:S(2)}, u32[]{:S(2)}) collective-permute-start(s32[256]{0:T(256)} %collective-permute-done.2), channel_id=1, source_target_pairs={{2,0},{4,2},{6,4},{8,6},{10,8},{12,10},{14,12},{3,1},{5,3},{7,5},{... | collective-permute-start | bytes 3080 | tf_op jit(solution)/shard_map/ppermute | solution.py:12
  69.9 84.3 %collective-permute-start.4 = (s32[256]{0:T(256)}, s32[256]{0:T(256)}, u32[]{:S(2)}, u32[]{:S(2)}) collective-permute-start(s32[256]{0:T(256)} %collective-permute-done), channel_id=1, source_target_pairs={{0,2},{2,4},{4,6},{6,8},{8,10},{10,12},{12,14},{1,3},{3,5},{5,7},{... | collective-permute-start | bytes 3080 | tf_op jit(solution)/shard_map/ppermute | solution.py:12
  129.1 11.9 %collective-permute-start.3 = (bf16[256,768]{1,0:T(8,128)(2,1)S(1)}, bf16[256,768]{1,0:T(8,128)(2,1)S(1)}, u32[]{:S(2)}, u32[]{:S(2)}) collective-permute-start(bf16[256,768]{1,0:T(8,128)(2,1)S(1)} %scatter_custom_fusion.3), channel_id=1, source_target_pairs={{2,0},{4,2},{6,4},{8,6},{10,8},{12,10},{14,12},{3,1},{5,3},{7,5},{... | collective-permute-start | bytes 1179656 | tf_op jit(solution)/shard_map/ppermute | solution.py:12
  130.4 18.0 %collective-permute-start.1 = (bf16[256,768]{1,0:T(8,128)(2,1)S(1)}, bf16[256,768]{1,0:T(8,128)(2,1)S(1)}, u32[]{:S(2)}, u32[]{:S(2)}) collective-permute-start(bf16[256,768]{1,0:T(8,128)(2,1)S(1)} %scatter_custom_fusion.3), channel_id=1, source_target_pairs={{0,2},{2,4},{4,6},{6,8},{8,10},{10,12},{12,14},{1,3},{3,5},{5,7},{... | collective-permute-start | bytes 1179656 | tf_op jit(solution)/shard_map/ppermute | solution.py:12
  136.1 1.4 copy-start.1
  141.0 12.7 %collective-permute-start.7 = (bf16[256,768]{1,0:T(8,128)(2,1)S(1)}, bf16[256,768]{1,0:T(8,128)(2,1)S(1)}, u32[]{:S(2)}, u32[]{:S(2)}) collective-permute-start(bf16[256,768]{1,0:T(8,128)(2,1)S(1)} %collective-permute-done.3), channel_id=1, source_target_pairs={{2,0},{4,2},{6,4},{8,6},{10,8},{12,10},{14,12},{3,1},{5,3},{7,5},{... | collective-permute-start | bytes 1179656 | tf_op jit(solution)/shard_map/ppermute | solution.py:12
  148.5 17.0 %collective-permute-start.5 = (bf16[256,768]{1,0:T(8,128)(2,1)S(1)}, bf16[256,768]{1,0:T(8,128)(2,1)S(1)}, u32[]{:S(2)}, u32[]{:S(2)}) collective-permute-start(bf16[256,768]{1,0:T(8,128)(2,1)S(1)} %collective-permute-done.1), channel_id=1, source_target_pairs={{0,2},{2,4},{4,6},{6,8},{8,10},{10,12},{12,14},{1,3},{3,5},{5,7},{... | collective-permute-start | bytes 1179656 | tf_op jit(solution)/shard_map/ppermute | solution.py:12
  153.3 12.2 %copy-start.6 = (pred[512]{0:T(512)(128)(4,1)S(1)}, pred[512]{0:T(512)(128)(4,1)}, u32[]{:S(2)}) copy-start(pred[512]{0:T(512)(128)(4,1)} %broadcast_compare_fusion.1) | copy-start | bytes 1540
  167.4 12.4 %all-to-all-start.2 = ((f32[8,1,64]{2,1,0:T(1,128)}), f32[8,1,64]{2,1,0:T(1,128)S(1)}, u32[]{:S(2)}, u32[]{:S(2)}) async-start(f32[8,1,64]{2,1,0:T(1,128)} %max.65), calls=%async_computation.2 | async-start | bytes 8192 | tf_op jit(solution)/shard_map/all_to_all | solution.py:103
Sparse Core Ops, SparseCore 0:
  26.8 95.4 all-reduce.1
Sparse Core Ops, SparseCore 1:
  49.1 11.1 all-gather.2
where the time goes:
time: 192 us; the launch traced here: 191 us
  waiting for transfers between devices  93.8 us (49%)
  starting transfers between devices  41.1 us (21%)
  local copies, waits for them, and re-layouts  18.3 us (10%)
  between operations  15.8 us (8%)
  other arithmetic  13.8 us (7%)
  matrix products  6.34 us (3%)
    psum x1, waiting for transfers between devices, body(): sums = lax.psum(partial_sums, ('blk', 'span'))  47.2 us
    ppermute x8, starting transfers between devices, passed_along(): lax.ppermute(value, axis, [(source, source + steps) for source in range(f...  24.3 us
    ppermute x8, waiting for transfers between devices, passed_along(): lax.ppermute(value, axis, [(source, source + steps) for source in range(f...  18.2 us
    all_to_all x1, waiting for transfers between devices, body(): lax.all_to_all(send_rows.reshape(owners, capacity, width), 'blk', split_a...  16.9 us
    all_to_all x1, starting transfers between devices, body(): lax.all_to_all(send_rows.reshape(owners, capacity, width), 'blk', split_a...  7.31 us
    all_to_all x1, starting transfers between devices, body(): lax.all_to_all(best.reshape(owners, capacity), 'blk', split_axis=0, conca...  5.92 us
    scatter x1, local copies, waits for them, and re-layouts, body(): jnp.zeros((share_limit, width), jnp.bfloat16).at[target]  5.74 us
    all_to_all x1, waiting for transfers between devices, body(): lax.all_to_all(best.reshape(owners, capacity), 'blk', split_axis=0, conca...  5.68 us
  transfers between devices with their start and end apart: 13, of which 7 were waited for; matrix products, arithmetic and copies ran while one was open for 13% of the time, Pallas kernels for 0%

commit v1 on v0

--- a/solution.py
+++ b/solution.py
@@ -2,6 +2,7 @@
 import jax.numpy as jnp
 from jax import lax
 from jax.sharding import PartitionSpec as P
+from jax.lax import all_gather
 
 GIANT_SPAN = 3
 
@@ -96,7 +97,8 @@
         (((0,), (0,)), ((), ())),
         preferred_element_type=jnp.float32,
     )
-    sums = lax.psum(partial_sums, ("blk", "span"))
+    current_block = all_gather(partial_sums, ("blk", "span"))
+    sums = jnp.sum(current_block, axis=0)
     length = jnp.sqrt(jnp.sum(sums * sums, axis=1, keepdims=True))
     direction = sums / jnp.maximum(length, 1.0)
     centroid_cosine = jnp.sum(unit.astype(jnp.float32) * direction[cluster], axis=1)

time: 192 us -> 157 us (0.82)
  waiting for transfers between devices: 93.8 us -> 45.6 us
  blocking collectives: 1.83 us -> 29.2 us
  starting transfers between devices: 41.1 us -> 30.9 us
    psum x1 -> x0, waiting for transfers between devices: 47.2 us -> none  [body(): sums = lax.psum(partial_sums, ('blk', 'span'))]
    all_to_all x0 -> x1, blocking collectives: none -> 27.4 us  [body(): lax.all_to_all(send_rows.reshape(owners, capacity, width), 'blk', split_a...]
    all_to_all x1 -> x0, waiting for transfers between devices: 16.9 us -> none  [body(): lax.all_to_all(send_rows.reshape(owners, capacity, width), 'blk', split_a...]
    ppermute x8, waiting for transfers between devices: 18.2 us -> 32.7 us  [passed_along(): lax.ppermute(value, axis, [(source, source + steps) for source in range(f...]
    all_to_all x1 -> x0, starting transfers between devices: 7.31 us -> none  [body(): lax.all_to_all(send_rows.reshape(owners, capacity, width), 'blk', split_a...]
    reduce_sum x0 -> x1, other arithmetic: none -> 3.18 us  [body(): sums = jnp.sum(current_block, axis=0)]
  transfers between devices with their start and end apart: 13 -> 12, of which waited for: 7 -> 4; matrix products, arithmetic and copies ran while one was open for 13% -> 15% of each run, Pallas kernels for 0% -> 0%
where the time goes in v1:
time: 157 us; the launch traced here: 156 us
  waiting for transfers between devices  45.6 us (29%)
  starting transfers between devices  30.9 us (20%)
  blocking collectives  29.2 us (19%)
  local copies, waits for them, and re-layouts  18.1 us (12%)
  between operations  14.4 us (9%)
  other arithmetic  12.6 us (8%)
  matrix products  5.67 us (4%)
    ppermute x8, waiting for transfers between devices, passed_along(): lax.ppermute(value, axis, [(source, source + steps) for source in range(f...  32.7 us
    all_to_all x1, blocking collectives, body(): lax.all_to_all(send_rows.reshape(owners, capacity, width), 'blk', split_a...  27.4 us
    ppermute x8, starting transfers between devices, passed_along(): lax.ppermute(value, axis, [(source, source + steps) for source in range(f...  22.7 us
    all_to_all x1, waiting for transfers between devices, body(): lax.all_to_all(best.reshape(owners, capacity), 'blk', split_axis=0, conca...  6.49 us
    all_to_all x1, waiting for transfers between devices, body(): lax.all_to_all(send_tags.reshape(owners, capacity), 'blk', split_axis=0,...  6.38 us
    scatter x1, local copies, waits for them, and re-layouts, body(): jnp.zeros((share_limit, width), jnp.bfloat16).at[target]  5.73 us
    all_to_all x1, starting transfers between devices, body(): lax.all_to_all(best.reshape(owners, capacity), 'blk', split_axis=0, conca...  4.57 us
    dot_general x5, matrix products, masked_scores(): lax.dot_general(left, right, (((1,), (1,)), ((), ())), preferred_element_...  4.56 us
  transfers between devices with their start and end apart: 12, of which 4 were waited for; matrix products, arithmetic and copies ran while one was open for 15% of the time, Pallas kernels for 0%

profile of v1, /device:TPU:0, one launch (start us, length us, event | category | flops | bytes accessed | tf_op | source)
XLA Modules:
  0.0 156.5 jit_solution(11686574984620200246)
XLA Ops:
  7.2 0.0 copy-start.2
  7.2 0.0 copy-start.1
  7.2 0.0 all-gather.5.cloned.1.call-start
  7.3 0.7 fusion.10
  8.0 0.6 reduce-window.15
  8.5 0.2 slice_reduce_fusion
  8.8 0.8 fusion.9
  9.6 0.7 compare_select_fusion.2
  10.3 1.2 fusion
  11.4 2.4 %scatter_custom_fusion.1 = bf16[512,768]{1,0:T(8,128)(2,1)S(1)} fusion(s32[256]{0:T(256)S(1)} %bitcast.53, bf16[]{:T(256)} %constant.23.clone.1, bf16[256,768]{1,0:T(8,128)(2,1)} %param.4, f32[256]{0:T(256)S(1)} %add_rsqrt_fusion), kind=kCustom, calls=%fused_computation.18 | custom fusion | flops 589824 | bytes 1180674 | tf_op jit(solution)/shard_map/scatter | solution.py:49
  13.9 27.4 %all_to_all.20 = bf16[8,64,768]{2,1,0:T(8,128)(2,1)} all-to-all(bf16[8,64,768]{2,1,0:T(8,128)(2,1)S(1)} %bitcast.44), channel_id=1, replica_groups=mesh['groups'=2,'blk'=8,'span'=2] {'blk'}, dimensions={0} | all-to-all | bytes 1572864 | tf_op jit(solution)/shard_map/all_to_all | solution.py:52
  41.2 0.0 all-gather.5.cloned.1.call-update
  41.2 0.0 all-gather.7.cloned.1.call-start
  41.3 0.2 select_reduce_fusion.5
  41.5 1.1 fusion.6
  42.6 0.0 all-gather.7.cloned.1.call-update
  42.7 1.4 scatter_custom_fusion
  44.1 0.7 all_to_all.13
  44.7 3.6 %all-to-all-start = ((s32[8,1,64]{2,1,0:T(1,128)}), s32[8,1,64]{2,1,0:T(1,128)S(1)}, u32[]{:S(2)}, u32[]{:S(2)}) async-start(s32[8,1,64]{2,1,0:T(1,128)} %all_to_all.13), calls=%async_computation | async-start | bytes 8192 | tf_op jit(solution)/shard_map/all_to_all | solution.py:59
  48.4 0.1 dynamic-slice_add_fusion
  48.4 6.4 %all-to-all-done = s32[8,1,64]{2,1,0:T(1,128)S(1)} async-done(((s32[8,1,64]{2,1,0:T(1,128)}), s32[8,1,64]{2,1,0:T(1,128)S(1)}, u32[]{:S(2)}, u32[]{:S(2)}) %all-to-all-start) | async-done | bytes 2080 | tf_op jit(solution)/shard_map/all_to_all | solution.py:59
  54.8 0.1 reshape.218
  54.9 1.8 %all-gather.1 = s32[2,1,512]{2,1,0:T(1,128)S(1)} all-gather(s32[1,1,512]{2,1,0:T(1,128)S(1)} %reshape.218), channel_id=1, replica_groups=mesh['groups'=2,'blk'=8,'span'=2] {'span'}, dimensions={0}, use_global_device_ids=true | all-gather | bytes 6144 | tf_op jit(solution)/shard_map/all_gather | solution.py:67
  56.8 0.3 reduce-window.19
  57.1 0.1 slice.19
  57.2 0.1 slice_reduce_fusion.1
  57.3 0.1 compare_select_fusion
  57.4 4.3 %scatter_custom_fusion.2 = s32[256]{0:T(256)S(1)} fusion(s32[1024]{0:T(1024)S(1)} %compare_select_fusion, s32[1024]{0:T(1024)S(1)} %bitcast.48, s32[]{:T(128)} %constant.19.clone.1), kind=kCustom, calls=%fused_computation.53 | custom fusion | bytes 1028 | tf_op jit(solution)/shard_map/scatter | solution.py:83
  61.7 2.5 %collective-permute-start = (s32[256]{0:T(256)S(1)}, s32[256]{0:T(256)S(1)}, u32[]{:S(2)}, u32[]{:S(2)}) collective-permute-start(s32[256]{0:T(256)S(1)} %scatter_custom_fusion.2), channel_id=1, source_target_pairs={{0,2},{2,4},{4,6},{6,8},{8,10},{10,12},{12,14},{1,3},{3,5},{5,7},{... | collective-permute-start | bytes 3080 | tf_op jit(solution)/shard_map/ppermute | solution.py:13
  64.1 1.3 collective-permute-start.2
  65.4 0.5 broadcast.121
  65.9 0.7 reduce.12
  66.6 0.1 eq.145
  66.7 5.7 %scatter_custom_fusion.3 = bf16[256,768]{1,0:T(8,128)(2,1)S(1)} fusion(s32[1024]{0:T(1024)S(1)} %compare_select_fusion, bf16[1024,768]{1,0:T(8,128)(2,1)} %all-gather.5.cloned.1.call-done, bf16[]{:T(256)} %constant.23.clone.1), kind=kCustom, calls=%fused_computation.21 | custom fusion | bytes 393728 | tf_op jit(solution)/shard_map/scatter | solution.py:82
  72.4 1.3 collective-permute-start.3
  73.7 0.0 collective-permute-done
  73.7 5.2 %collective-permute-start.4 = (s32[256]{0:T(256)S(1)}, s32[256]{0:T(256)S(1)}, u32[]{:S(2)}, u32[]{:S(2)}) collective-permute-start(s32[256]{0:T(256)S(1)} %collective-permute-done), channel_id=1, source_target_pairs={{0,2},{2,4},{4,6},{6,8},{8,10},{10,12},{12,14},{1,3},{3,5},{5,7},{... | collective-permute-start | bytes 3080 | tf_op jit(solution)/shard_map/ppermute | solution.py:13
  78.9 0.0 collective-permute-done.2
  78.9 1.3 collective-permute-start.6
  80.2 5.5 %collective-permute-start.1 = (bf16[256,768]{1,0:T(8,128)(2,1)S(1)}, bf16[256,768]{1,0:T(8,128)(2,1)S(1)}, u32[]{:S(2)}, u32[]{:S(2)}) collective-permute-start(bf16[256,768]{1,0:T(8,128)(2,1)S(1)} %scatter_custom_fusion.3), channel_id=1, source_target_pairs={{0,2},{2,4},{4,6},{6,8},{8,10},{10,12},{12,14},{1,3},{3,5},{5,7},{... | collective-permute-start | bytes 1179656 | tf_op jit(solution)/shard_map/ppermute | solution.py:13
  85.7 2.8 %select_reduce_fusion = f32[512]{0:T(512)S(1)} fusion(bf16[512,768]{1,0:T(8,128)(2,1)S(1)} %bitcast.38, bf16[1024,768]{1,0:T(8,128)(2,1)} %all-gather.5.cloned.1.call-done, s32[1024]{0:T(1024)S(1)} %bitcast.49, s32[512]{0:T(512)S(1)} %iota_add_fusion, s32[512]{0:T(512)S(1)} %eq.145, pred[512]{0:T(512)(128)(4,1)S(1)} %broadcast_compare_fusion.1), kind=kOutput, calls=%fused_computation.6 | convolution fusion | flops 808451584 | bytes 2370048 | tf_op jit(solution)/shard_map/dot_general | solution.py:23
  88.5 0.0 collective-permute-done.3
  88.5 1.3 collective-permute-start.7
  89.8 0.4 fusion.18
  90.2 22.4 %collective-permute-done.1 = bf16[256,768]{1,0:T(8,128)(2,1)S(1)} collective-permute-done((bf16[256,768]{1,0:T(8,128)(2,1)S(1)}, bf16[256,768]{1,0:T(8,128)(2,1)S(1)}, u32[]{:S(2)}, u32[]{:S(2)}) %collective-permute-start.1) | collective-permute-done | bytes 393248 | tf_op jit(solution)/shard_map/ppermute | solution.py:13
  112.7 4.4 %collective-permute-start.5 = (bf16[256,768]{1,0:T(8,128)(2,1)S(1)}, bf16[256,768]{1,0:T(8,128)(2,1)S(1)}, u32[]{:S(2)}, u32[]{:S(2)}) collective-permute-start(bf16[256,768]{1,0:T(8,128)(2,1)S(1)} %collective-permute-done.1), channel_id=1, source_target_pairs={{0,2},{2,4},{4,6},{6,8},{8,10},{10,12},{12,14},{1,3},{3,5},{5,7},{... | collective-permute-start | bytes 1179656 | tf_op jit(solution)/shard_map/ppermute | solution.py:13
  117.1 0.4 fusion.17
  117.5 0.0 collective-permute-done.7
  117.5 0.4 fusion.19
  117.9 0.0 collective-permute-done.4
  117.9 10.3 %collective-permute-done.5 = bf16[256,768]{1,0:T(8,128)(2,1)S(1)} collective-permute-done((bf16[256,768]{1,0:T(8,128)(2,1)S(1)}, bf16[256,768]{1,0:T(8,128)(2,1)S(1)}, u32[]{:S(2)}, u32[]{:S(2)}) %collective-permute-start.5) | collective-permute-done | bytes 393248 | tf_op jit(solution)/shard_map/ppermute | solution.py:13
  128.2 0.6 select_reduce_fusion.4
  128.8 0.7 max.65
  129.5 4.6 %all-to-all-start.2 = ((f32[8,1,64]{2,1,0:T(1,128)}), f32[8,1,64]{2,1,0:T(1,128)S(1)}, u32[]{:S(2)}, u32[]{:S(2)}) async-start(f32[8,1,64]{2,1,0:T(1,128)} %max.65), calls=%async_computation.2 | async-start | bytes 8192 | tf_op jit(solution)/shard_map/all_to_all | solution.py:105
  134.0 6.5 %all-to-all-done.2 = f32[8,1,64]{2,1,0:T(1,128)S(1)} async-done(((f32[8,1,64]{2,1,0:T(1,128)}), f32[8,1,64]{2,1,0:T(1,128)S(1)}, u32[]{:S(2)}, u32[]{:S(2)}) %all-to-all-start.2) | async-done | bytes 2080 | tf_op jit(solution)/shard_map/all_to_all | solution.py:105
  140.5 0.5 broadcast.122
  141.0 0.7 reduce.13
  141.7 0.1 reshape.165
  141.8 2.5 %gather_fusion = f32[256]{0:T(256)} fusion(f32[512]{0:T(512)S(1)} %reshape.165, s32[1024]{0:T(1024)S(1)} %pad_clamp_fusion.1), kind=kCustom, calls=%fused_computation | custom fusion | bytes 3072 | tf_op jit(solution)/shard_map/gather | solution.py:108
  144.3 3.2 %reduce_sum.62 = f32[128,768]{1,0:T(8,128)S(1)} reduce(f32[16,128,768]{2,1,0:T(8,128)} %bitcast.43, f32[]{:T(128)} %constant.24.clone.1), dimensions={0}, to_apply=%region_16.17 | reduce | flops 1474560 | bytes 6684676 | tf_op jit(solution)/shard_map/reduce_sum | solution.py:101
  147.5 0.1 multiply_reduce_fusion.1
  147.6 0.1 broadcast_divide_fusion
  147.7 1.1 gather_fusion.1
  148.8 0.8 multiply_reduce_fusion
  (25 shorter events, 0.2 us)
Async XLA Ops:
  7.2 34.1 %copy-start.2 = (s32[256,1]{0,1:T(1,128)S(1)}, s32[256,1]{0,1:T(1,128)}, u32[]{:S(2)}) copy-start(s32[256,1]{0,1:T(1,128)} %param.5) | copy-start | bytes 3076
  7.2 34.3 %copy-start.1 = (bf16[256,768]{1,0:T(8,128)(2,1)S(1)}, bf16[256,768]{1,0:T(8,128)(2,1)}, u32[]{:S(2)}) copy-start(bf16[256,768]{1,0:T(8,128)(2,1)} %param.4) | copy-start | bytes 1179652
  7.2 34.1 %copy-start.3 = (s32[256]{0:T(256)S(1)}, s32[256]{0:T(256)}, u32[]{:S(2)}) copy-start(s32[256]{0:T(256)} %param.6) | copy-start | bytes 3076
  7.2 34.1 %copy-start.4 = (s32[128]{0:T(128)S(1)}, s32[128]{0:T(128)}, u32[]{:S(2)}) copy-start(s32[128]{0:T(128)} %param.7) | copy-start | bytes 1540
  7.2 59.5 %all-gather.5.cloned.1.call-start = ((), (), s32[]{:S(2)}) async-start(), calls=%async_computation.3 | async-start | bytes 2359296 | tf_op jit(solution)/shard_map/all_gather | solution.py:66
  41.2 44.5 %copy-start = (bf16[8,64,768]{2,1,0:T(8,128)(2,1)S(1)}, bf16[8,64,768]{2,1,0:T(8,128)(2,1)}, u32[]{:S(2)}) copy-start(bf16[8,64,768]{2,1,0:T(8,128)(2,1)} %all_to_all.20) | copy-start | bytes 2359300
  41.2 103.0 %all-gather.7.cloned.1.call-start = ((), (), s32[]{:S(2)}) async-start(), calls=%async_computation.4 | async-start | bytes 6684672 | tf_op jit(solution)/shard_map/all_gather | solution.py:100
  44.7 10.1 %all-to-all-start = ((s32[8,1,64]{2,1,0:T(1,128)}), s32[8,1,64]{2,1,0:T(1,128)S(1)}, u32[]{:S(2)}, u32[]{:S(2)}) async-start(s32[8,1,64]{2,1,0:T(1,128)} %all_to_all.13), calls=%async_computation | async-start | bytes 8192 | tf_op jit(solution)/shard_map/all_to_all | solution.py:59
  61.7 12.1 %collective-permute-start = (s32[256]{0:T(256)S(1)}, s32[256]{0:T(256)S(1)}, u32[]{:S(2)}, u32[]{:S(2)}) collective-permute-start(s32[256]{0:T(256)S(1)} %scatter_custom_fusion.2), channel_id=1, source_target_pairs={{0,2},{2,4},{4,6},{6,8},{8,10},{10,12},{12,14},{1,3},{3,5},{5,7},{... | collective-permute-start | bytes 3080 | tf_op jit(solution)/shard_map/ppermute | solution.py:13
  64.1 14.8 %collective-permute-start.2 = (s32[256]{0:T(256)S(1)}, s32[256]{0:T(256)S(1)}, u32[]{:S(2)}, u32[]{:S(2)}) collective-permute-start(s32[256]{0:T(256)S(1)} %scatter_custom_fusion.2), channel_id=1, source_target_pairs={{2,0},{4,2},{6,4},{8,6},{10,8},{12,10},{14,12},{3,1},{5,3},{7,5},{... | collective-permute-start | bytes 3080 | tf_op jit(solution)/shard_map/ppermute | solution.py:13
  72.4 16.1 %collective-permute-start.3 = (bf16[256,768]{1,0:T(8,128)(2,1)S(1)}, bf16[256,768]{1,0:T(8,128)(2,1)S(1)}, u32[]{:S(2)}, u32[]{:S(2)}) collective-permute-start(bf16[256,768]{1,0:T(8,128)(2,1)S(1)} %scatter_custom_fusion.3), channel_id=1, source_target_pairs={{2,0},{4,2},{6,4},{8,6},{10,8},{12,10},{14,12},{3,1},{5,3},{7,5},{... | collective-permute-start | bytes 1179656 | tf_op jit(solution)/shard_map/ppermute | solution.py:13
  73.7 44.1 %collective-permute-start.4 = (s32[256]{0:T(256)S(1)}, s32[256]{0:T(256)S(1)}, u32[]{:S(2)}, u32[]{:S(2)}) collective-permute-start(s32[256]{0:T(256)S(1)} %collective-permute-done), channel_id=1, source_target_pairs={{0,2},{2,4},{4,6},{6,8},{8,10},{10,12},{12,14},{1,3},{3,5},{5,7},{... | collective-permute-start | bytes 3080 | tf_op jit(solution)/shard_map/ppermute | solution.py:13
  78.9 39.0 %collective-permute-start.6 = (s32[256]{0:T(256)S(1)}, s32[256]{0:T(256)S(1)}, u32[]{:S(2)}, u32[]{:S(2)}) collective-permute-start(s32[256]{0:T(256)S(1)} %collective-permute-done.2), channel_id=1, source_target_pairs={{2,0},{4,2},{6,4},{8,6},{10,8},{12,10},{14,12},{3,1},{5,3},{7,5},{... | collective-permute-start | bytes 3080 | tf_op jit(solution)/shard_map/ppermute | solution.py:13
  80.2 32.4 %collective-permute-start.1 = (bf16[256,768]{1,0:T(8,128)(2,1)S(1)}, bf16[256,768]{1,0:T(8,128)(2,1)S(1)}, u32[]{:S(2)}, u32[]{:S(2)}) collective-permute-start(bf16[256,768]{1,0:T(8,128)(2,1)S(1)} %scatter_custom_fusion.3), channel_id=1, source_target_pairs={{0,2},{2,4},{4,6},{6,8},{8,10},{10,12},{12,14},{1,3},{3,5},{5,7},{... | collective-permute-start | bytes 1179656 | tf_op jit(solution)/shard_map/ppermute | solution.py:13
  88.5 28.9 %collective-permute-start.7 = (bf16[256,768]{1,0:T(8,128)(2,1)S(1)}, bf16[256,768]{1,0:T(8,128)(2,1)S(1)}, u32[]{:S(2)}, u32[]{:S(2)}) collective-permute-start(bf16[256,768]{1,0:T(8,128)(2,1)S(1)} %collective-permute-done.3), channel_id=1, source_target_pairs={{2,0},{4,2},{6,4},{8,6},{10,8},{12,10},{14,12},{3,1},{5,3},{7,5},{... | collective-permute-start | bytes 1179656 | tf_op jit(solution)/shard_map/ppermute | solution.py:13
  112.7 15.5 %collective-permute-start.5 = (bf16[256,768]{1,0:T(8,128)(2,1)S(1)}, bf16[256,768]{1,0:T(8,128)(2,1)S(1)}, u32[]{:S(2)}, u32[]{:S(2)}) collective-permute-start(bf16[256,768]{1,0:T(8,128)(2,1)S(1)} %collective-permute-done.1), channel_id=1, source_target_pairs={{0,2},{2,4},{4,6},{6,8},{8,10},{10,12},{12,14},{1,3},{3,5},{5,7},{... | collective-permute-start | bytes 1179656 | tf_op jit(solution)/shard_map/ppermute | solution.py:13
  129.5 11.1 %all-to-all-start.2 = ((f32[8,1,64]{2,1,0:T(1,128)}), f32[8,1,64]{2,1,0:T(1,128)S(1)}, u32[]{:S(2)}, u32[]{:S(2)}) async-start(f32[8,1,64]{2,1,0:T(1,128)} %max.65), calls=%async_computation.2 | async-start | bytes 8192 | tf_op jit(solution)/shard_map/all_to_all | solution.py:105
Sparse Core Ops, SparseCore 0:
  41.4 8.7 all-gather.4
  52.5 89.2 all-gather.6
